TPU v7x, 256 devices: a whole 4x4x8 slice. The times are simulated.
256 devices in a mesh: group: 8 (over z), shard: 32 (over x, y, core).
Axes of the slice: x: 4, y: 4, z: 8, core: 2. Of those that a mesh axis runs over, the one named last changes fastest.
Arguments:
- queries: bfloat16 [1536, 1024], P(('group', 'shard')), may hold values from -12 to 12
- candidates: bfloat16 [1048576, 1024], P(('group', 'shard')), may hold values from -4 to 4
- targets: int32 [1536], replicated, may hold values from 0 to 1048575
Outputs:
- losses: float32 [1536], replicated
- mean_loss: float32 [], replicated
All inputs are finite; a program needn't handle non-finite values.
Results may differ from a plain program's by a relative error of at most 0.0003.
Values may be sent and summed in bfloat16 or wider, within the bound.
A program may use at most 64 MiB of HBM per device.

v0:
```python
import math

import jax
import jax.numpy as jnp
from jax import lax
from jax.sharding import Mesh
from jax.sharding import PartitionSpec as P

SHARD = ("shard_0", "shard_1", "shard_2")
GROUP_SHARD = ("group", "shard_0", "shard_1", "shard_2")


def laid_out(tiles, dim):
    shape = list(tiles.shape[1:])
    shape[dim] *= tiles.shape[0]
    return jnp.moveaxis(tiles, 0, dim).reshape(shape)


def gather_in_order(value, axes, order):
    tiles = value[None]
    for k in order:
        tiles = lax.all_gather(tiles, axes[k], axis=0, tiled=True)
    held = [lax.axis_size(axes[k]) for k in reversed(order)]
    tiles = tiles.reshape(*held, *value.shape)
    turned = sorted(range(len(order)), key=lambda place: order[len(order) - 1 - place])
    return tiles.transpose(*turned, *range(len(order), tiles.ndim)).reshape(-1, *value.shape)


def gather_axes(value, axes, order, dim):
    return laid_out(gather_in_order(value, axes, order), dim)


def from_everyone(value, axis):
    copies = jnp.broadcast_to(value, (lax.axis_size(axis), *value.shape))
    return lax.all_to_all(copies, axis, split_axis=0, concat_axis=0, tiled=True)


def collected_together(value, axis):
    leaves = jax.tree.leaves(value)
    order = sorted(range(len(leaves)), key=lambda k: -leaves[k].size)
    width = (1, *leaves[order[0]].shape)[-1]
    lines = [
        jnp.pad(leaves[k].reshape(-1), (0, -leaves[k].size % width)).reshape(-1, width)
        for k in order
    ]
    both, at, found = (from_everyone(jnp.concatenate(lines), axis), 0, {})
    for k, line in zip(order, lines):
        share = both[:, at : at + len(line)].reshape(len(both), -1)
        found[k] = share[:, : leaves[k].size].reshape(-1, *leaves[k].shape)
        at += len(line)
    numbers = iter(range(len(leaves)))
    return jax.tree.map(lambda _: found[next(numbers)], value)


def folded_in_pairs(pieces, combine):
    while len(jax.tree.leaves(pieces)[0]) > 1:
        pieces = jax.vmap(combine)(
            *(jax.tree.map(lambda part: part[side::2], pieces) for side in (0, 1))
        )
    return jax.tree.map(lambda part: part[0], pieces)


def combined_all(value, axis, combine):
    pieces = collected_together(value, axis)
    return folded_in_pairs(pieces, combine)


def once_a_type(value, axis):
    leaves, found = (jax.tree.leaves(value), {})
    for leading, a in enumerate(leaves):
        if leading not in found:
            alike = [k for k, b in enumerate(leaves) if b.dtype == a.dtype]
            got = (
                collected_together([leaves[k] for k in alike], axis)
                if len(alike) > 1
                else [from_everyone(a, axis)]
            )
            for k, b in zip(alike, got):
                found[k] = b
    numbers = iter(range(len(leaves)))
    return jax.tree.map(lambda _: found[next(numbers)], value)


def merged(value, axis, combine):
    pieces = once_a_type(value, axis)
    return folded_in_pairs(pieces, combine)


def combine(first, second):
    top = jnp.maximum(first[0], second[0])
    total = first[1] * jnp.exp(first[0] - top) + second[1] * jnp.exp(second[0] - top)
    return (top, total, first[2] + second[2])


def score_rows(piece, candidates, chosen_targets, owner):
    rows = candidates.shape[0]
    local = chosen_targets - owner * rows
    owned = (local >= 0) & (local < rows)
    chosen = jnp.take(candidates, jnp.clip(local, 0, rows - 1), axis=0)
    products = jnp.sum(piece.astype(jnp.float32) * chosen.astype(jnp.float32), axis=1)
    picked = jnp.where(owned, products, jnp.float32(0.0))
    count = piece.shape[0]
    block = math.gcd(count, 512)
    panels = piece.reshape(count // block, block, piece.shape[1])

    def score_panel(panel):
        scores = jnp.dot(panel, candidates.T, preferred_element_type=jnp.float32)
        peak = jnp.max(scores, axis=1)
        return (peak, jnp.sum(jnp.exp(scores - peak[:, None]), axis=1))

    peaks, sums = lax.map(score_panel, panels)
    return (peaks.reshape(count), sums.reshape(count), picked)


def on_device(queries, candidates, targets):
    owner = lax.axis_index("group") * lax.axis_size(SHARD) + lax.axis_index(SHARD)
    every = gather_axes(queries, GROUP_SHARD, (1, 0, 2, 3), 0)
    top, total, picked = score_rows(every, candidates, targets, owner)
    inner = combined_all((top, total, picked), SHARD, combine)
    top, total, picked = merged(inner, "group", combine)
    losses = top + jnp.log(total) - picked
    return (losses, jnp.mean(losses))


def solution(mesh):
    finer = Mesh(
        mesh.devices.reshape(mesh.shape["group"], 4, 4, 2),
        ("group", "shard_0", "shard_1", "shard_2"),
    )
    in_specs = (P(GROUP_SHARD, None), P(GROUP_SHARD, None), P())
    out_specs = (P(), P())
    return jax.shard_map(
        on_device, mesh=finer, in_specs=in_specs, out_specs=out_specs, check_vma=False
    )
```

profile of v0, /device:TPU:1, one launch (start us, length us, event | category | flops | bytes accessed | tf_op | source)
XLA Modules:
  0.0 195.4 jit_solution(15849809175005774843)
XLA Ops:
  7.2 10.4 %all-gather.1 = bf16[4,6,1024]{2,1,0:T(8,128)(2,1)S(1)} all-gather(bf16[1,6,1024]{2,1,0:T(8,128)(2,1)} %bitcast.56), channel_id=2, replica_groups=mesh['group'=8,'shard_0'=4,'shard_1'=4,'shard_2'=2] {'shard_0'}, dimensions={0}, use_global_device_ids=true | all-gather | bytes 61440 | tf_op jit(solution)/shard_map/all_gather | solution.py:22
  17.6 23.3 %all_gather.13 = bf16[32,6,1024]{2,1,0:T(8,128)(2,1)S(1)} all-gather(bf16[4,6,1024]{2,1,0:T(8,128)(2,1)S(1)} %all-gather.1), channel_id=1, replica_groups=mesh['group'=8,'shard_0'=4,'shard_1'=4,'shard_2'=2] {'group'}, dimensions={0}, use_global_device_ids=true | all-gather | bytes 442368 | tf_op jit(solution)/shard_map/all_gather | solution.py:22
  40.9 1.0 copy.36
  41.9 36.5 %all-gather.5.cloned.1.call-done = bf16[128,6,1024]{2,0,1:T(8,128)(2,1)} async-done(((bf16[32,6,1024]{2,0,1:T(8,128)(2,1)}), bf16[128,6,1024]{2,0,1:T(8,128)(2,1)}) %all-gather.5.cloned.1.call-update) | async-done | bytes 1572880 | tf_op jit(solution)/shard_map/all_gather | solution.py:22
  78.5 0.7 compare_and_fusion
  79.2 11.6 %gather_fusion = bf16[1536,1024]{1,0:T(8,128)(2,1)S(1)} fusion(bf16[4096,1024]{1,0:T(8,128)(2,1)} %param.6, s32[2048]{0:T(1024)S(1)} %pad_clamp_fusion), kind=kCustom, calls=%fused_computation | custom fusion | bytes 6297600 | tf_op jit(solution)/shard_map/jit(_take)/gather | solution.py:99
  90.8 2.9 %gather.7 = bf16[8,4,4,2,6,1024]{5,4,3,2,1,0:T(8,128)(2,1)} reshape(bf16[1536,1024]{1,0:T(8,128)(2,1)S(1)} %gather_fusion) | data formatting | bytes 6291456 | tf_op jit(solution)/shard_map/jit(_take)/gather | solution.py:99
  93.9 0.6 copy.38
  94.5 4.1 %all-gather.7.cloned.1.call-done = bf16[256,6,1024]{2,0,1:T(8,128)(2,1)} async-done(((bf16[128,6,1024]{2,0,1:T(8,128)(2,1)}), bf16[256,6,1024]{2,0,1:T(8,128)(2,1)}) %all-gather.7.cloned.1.call-update) | async-done | bytes 3145744 | tf_op jit(solution)/shard_map/all_gather | solution.py:22
  98.6 4.0 %reshape.57 = bf16[2,4,8,4,6,1024]{5,3,2,1,0,4:T(4,128)(2,1)S(1)} reshape(bf16[256,6,1024]{2,0,1:T(8,128)(2,1)} %all-gather.7.cloned.1.call-done) | data formatting | bytes 6291456 | tf_op jit(solution)/shard_map/reshape | solution.py:24
  102.6 7.8 %multiply_reduce_fusion = f32[8,4,4,2,6]{1,0,2,3,4:T(8,128)S(1)} fusion(bf16[8,4,4,2,6,1024]{5,4,3,2,1,0:T(8,128)(2,1)} %gather.7, pred[8,4,4,2,6]{1,0,2,3,4:T(8,128)(4,1)S(1)} %copy.38, bf16[2,4,8,4,6,1024]{5,3,2,1,0,4:T(4,128)(2,1)S(1)} %reshape.57), kind=kLoop, calls=%fused_computation.6 | loop fusion | flops 7862784 | bytes 6299136 | tf_op jit(solution)/shard_map/reduce_sum | solution.py:100
  110.4 0.5 copy.40
  111.2 3.7 %copy.37 = bf16[8,4,4,2,6,1024]{5,4,3,2,1,0:T(8,128)(2,1)} copy(bf16[8,4,4,2,6,1024]{5,1,0,2,3,4:T(4,128)(2,1)S(1)} %bitcast.43) | data formatting | bytes 6291456 | tf_op jit(solution)/shard_map/transpose | solution.py:26
  115.0 4.9 %reshape_reshape_reshape.3 = bf16[3,512,1024]{2,1,0:T(8,128)(2,1)S(1)} reshape(bf16[8,4,4,2,6,1024]{5,4,3,2,1,0:T(8,128)(2,1)} %copy.37) | data formatting | bytes 6291456 | tf_op jit(solution)/shard_map/reshape;reshape;reshape | solution.py:104
  119.8 25.6 %while.12 = (s32[]{:T(128)}, f32[3,512]{1,0:T(4,128)S(1)}, f32[3,512]{1,0:T(4,128)S(1)}, bf16[3,512,1024]{2,1,0:T(8,128)(2,1)S(1)}, bf16[4096,1024]{1,0:T(8,128)(2,1)}, /*index=5*/s32[]{:T(128)}, s32[]{:T(128)}) while((s32[]{:T(128)}, f32[3,512]{1,0:T(4,128)S(1)}, f32[3,512]{1,0:T(4,128)S(1)}, bf16[3,512,1024]{2,1,0:T(8,128)(2,1)S(1)}, ...), condition=%wide.region_3.4_spmd, body=%wide.region_0.0_spmd.sunk | while | flops 4301257728 | bytes 26228824 | solution.py:111
  119.9 7.1 %fusion.16 = (f32[512]{0:T(512)S(1)}, f32[512,4096]{1,0:T(8,128)S(1)}) fusion(bf16[4096,1024]{1,0:T(8,128)(2,1)} %get-tuple-element.123, bf16[3,512,1024]{2,1,0:T(8,128)(2,1)S(1)} %get-tuple-element.122, s32[]{:T(128)} %get-tuple-element.112), kind=kOutput, calls=%fused_computation.39.clone.1 | convolution fusion | flops 4297063936 | bytes 17827844 | tf_op jit(solution)/shard_map/while/body/eval_jaxpr/dot_general | solution.py:107
  127.0 1.3 exponential_reduce_fusion.2
  128.4 7.1 %fusion.16 = (f32[512]{0:T(512)S(1)}, f32[512,4096]{1,0:T(8,128)S(1)}) fusion(bf16[4096,1024]{1,0:T(8,128)(2,1)} %get-tuple-element.123, bf16[3,512,1024]{2,1,0:T(8,128)(2,1)S(1)} %get-tuple-element.122, s32[]{:T(128)} %get-tuple-element.112), kind=kOutput, calls=%fused_computation.39.clone.1 | convolution fusion | flops 4297063936 | bytes 17827844 | tf_op jit(solution)/shard_map/while/body/eval_jaxpr/dot_general | solution.py:107
  135.5 1.3 exponential_reduce_fusion.2
  136.9 7.1 %fusion.16 = (f32[512]{0:T(512)S(1)}, f32[512,4096]{1,0:T(8,128)S(1)}) fusion(bf16[4096,1024]{1,0:T(8,128)(2,1)} %get-tuple-element.123, bf16[3,512,1024]{2,1,0:T(8,128)(2,1)S(1)} %get-tuple-element.122, s32[]{:T(128)} %get-tuple-element.112), kind=kOutput, calls=%fused_computation.39.clone.1 | convolution fusion | flops 4297063936 | bytes 17827844 | tf_op jit(solution)/shard_map/while/body/eval_jaxpr/dot_general | solution.py:107
  144.0 1.3 exponential_reduce_fusion.2
  145.6 20.8 %all_to_all.10 = f32[32,3,1536]{2,1,0:T(4,128)S(1)} all-to-all(f32[32,3,1536]{2,1,0:T(4,128)S(1)} %broadcast_in_dim.41), channel_id=1, replica_groups=mesh['group'=8,'shard_0'=4,'shard_1'=4,'shard_2'=2] {'shard_0','shard_1'..., dimensions={0} | all-to-all | bytes 1179648 | tf_op jit(solution)/shard_map/all_to_all | solution.py:35
  168.0 17.4 %all_to_all.11 = f32[8,3,1536]{2,1,0:T(4,128)S(1)} all-to-all(f32[8,3,1536]{2,1,0:T(4,128)S(1)} %broadcast_in_dim.42), channel_id=1, replica_groups=mesh['group'=8,'shard_0'=4,'shard_1'=4,'shard_2'=2] {'group'}, dimensions={0} | all-to-all | bytes 294912 | tf_op jit(solution)/shard_map/all_to_all | solution.py:35
  186.0 0.7 fusion.8
  (82 shorter events, 2.9 us)
Async XLA Ops:
  7.2 71.3 %all-gather.5.cloned.1.call-start = ((), (), s32[]{:S(2)}) async-start(), calls=%async_computation.2 | async-start | bytes 1966080 | tf_op jit(solution)/shard_map/all_gather | solution.py:22
  41.9 56.7 %all-gather.7.cloned.1.call-start = ((), (), s32[]{:S(2)}) async-start(), calls=%async_computation.3 | async-start | bytes 4718592 | tf_op jit(solution)/shard_map/all_gather | solution.py:22
  102.6 8.6 %copy-start = (s32[1536]{0:T(1024)S(1)}, s32[1536]{0:T(1024)}, u32[]{:S(2)}) copy-start(s32[1536]{0:T(1024)} %param.7) | copy-start | bytes 18436
Sparse Core Ops, SparseCore 0:
  42.0 36.4 all-gather.4
  80.2 18.3 all-gather.6
where the time goes:
time: 196 us; the launch traced here: 195 us
  blocking collectives  71.9 us (37%)
  waiting for transfers between devices  40.6 us (21%)
  local copies, waits for them, and re-layouts  31.7 us (16%)
  matrix products  21.4 us (11%)
  between operations  16.2 us (8%)
  other arithmetic  13.4 us (7%)
    all_gather x2, waiting for transfers between devices, gather_in_order(): tiles = lax.all_gather(tiles, axes[k], axis=0, tiled=True)  40.6 us
    all_to_all x2, blocking collectives, from_everyone(): return lax.all_to_all(copies, axis, split_axis=0, concat_axis=0, tiled=True)  38.3 us
    all_gather x2, blocking collectives, gather_in_order(): tiles = lax.all_gather(tiles, axes[k], axis=0, tiled=True)  33.7 us
    dot_general x3, matrix products, score_panel(): scores = jnp.dot(panel, candidates.T, preferred_element_type=jnp.float32)  21.4 us
    gather x2, local copies, waits for them, and re-layouts, score_rows(): chosen = jnp.take(candidates, jnp.clip(local, 0, rows - 1), axis=0)  14.5 us
    reduce_sum x1, other arithmetic, score_rows(): jnp.sum(piece.astype(jnp.float32) * chosen.astype(jnp.float32), axis=1)  7.8 us
    another operation x1, local copies, waits for them, and re-layouts, score_rows(): panels = piece.reshape(count // block, block, piece.shape[1])  4.87 us
    reshape x1, local copies, waits for them, and re-layouts, gather_in_order(): tiles = tiles.reshape(*held, *value.shape)  4.01 us
  transfers between devices with their start and end apart: 2, of which 2 were waited for; matrix products, arithmetic and copies ran while one was open for 8% of the time, Pallas kernels for 0%

commit v1 on v0

v1 whole, which is shorter than its diff:
```python
import functools

import jax
import jax.numpy as jnp
from jax import lax
from jax.experimental import pallas as pl
from jax.experimental.pallas import tpu as pltpu
from jax.sharding import Mesh
from jax.sharding import PartitionSpec as P

SHARD = ("x", "y", "core")
EVERY = ("group",) + SHARD
MESH = pl.DeviceIdType.MESH
NZ, NX, NY = 8, 4, 4
PLANE = NX * NY * 2
LANES = 128
CHUNK = 256
ROWS = 1024
LOWEST = -3.0e38

SLOTS = (
    ("o", 0, 0), ("o", 1, 0), ("o", 3, 0), ("o", 0, 1), ("o", 0, 3), ("m", 0, 0),
    ("o", 2, 0), ("m", 1, 0), ("m", 3, 0), ("m", 0, 1), ("m", 0, 3),
    ("m", 2, 0), ("o", 1, 1), ("o", 3, 1), ("o", 1, 3), ("o", 3, 3),
    ("o", 2, 1), ("o", 2, 3), ("m", 1, 1), ("m", 3, 1), ("m", 1, 3), ("m", 3, 3),
    ("m", 2, 1), ("m", 2, 3), ("o", 0, 2), ("o", 1, 2), ("o", 2, 2),
    ("o", 3, 2), ("m", 0, 2), ("m", 1, 2), ("m", 2, 2), ("m", 3, 2),
)
PLACE = {slot: k for k, slot in enumerate(SLOTS)}
ARRIVALS = {
    (0, 0): (("o", 1, 0), ("o", 3, 0), ("o", 0, 1), ("o", 0, 3), ("m", 0, 0)),
    (0, 2): (("o", 2, 0),),
    (1, 0): (("m", 1, 0), ("m", 3, 0), ("m", 0, 1), ("m", 0, 3)),
    (1, 2): (("o", 1, 1), ("o", 3, 1), ("o", 1, 3), ("o", 3, 3)),
    (2, 0): (("m", 2, 0),),
    (2, 2): (("o", 2, 1), ("o", 2, 3)),
    (3, 0): (("m", 1, 1), ("m", 3, 1), ("m", 1, 3), ("m", 3, 3)),
    (3, 2): (("o", 0, 2), ("o", 1, 2)),
    (4, 0): (("m", 2, 1), ("m", 2, 3), ("o", 2, 2)),
    (4, 2): (("o", 3, 2),),
    (5, 0): (("m", 0, 2), ("m", 1, 2), ("m", 2, 2), ("m", 3, 2)),
}


def folded(block, count, top, total, picked, wanted, first):
    tops = [top, None, None, None]
    for r in range(count):
        v = block[8 * r : 8 * r + 8, :]
        tops[r % 4] = v if tops[r % 4] is None else jnp.maximum(tops[r % 4], v)
    new = jnp.maximum(jnp.maximum(tops[0], tops[1]), jnp.maximum(tops[2], tops[3]))
    sums = [total * jnp.exp(top - new), None, None, None]
    for r in range(count):
        v = block[8 * r : 8 * r + 8, :]
        e = jnp.exp(v - new)
        sums[r % 4] = e if sums[r % 4] is None else sums[r % 4] + e
        picked = jnp.where(wanted == first + r, v, picked)
    return new, (sums[0] + sums[1]) + (sums[2] + sums[3]), picked


def merged(pieces):
    top = jnp.max(pieces[:, 0:1, :], axis=0)
    total = jnp.sum(jnp.exp(pieces[:, 0:1, :] - top[None]), axis=0)
    return top + jnp.log(total), jnp.sum(pieces[:, 1:2, :], axis=0)


def kernel(
    q_ref, t_ref, c_hbm, out_ref,
    zbuf, qall, cbuf, sbuf, trel, res, part, inbox, zin, outall,
    c_sem, zs_sem, zr_sem, send_sem, own_sem, mate_sem,
    rs_sem, rr_sem, gs_sem, gr_sem, as_sem, ar_sem,
):
    z, x, y, c = (lax.axis_index(a) for a in EVERY)
    per = q_ref.shape[0]
    block = NZ * per
    n_cand = cbuf.shape[0]
    steps = n_cand // ROWS
    me = (x * NY + y) * 2 + c
    base = (z * PLANE + me) * n_cand

    loads = [
        pltpu.make_async_copy(
            c_hbm.at[pl.ds(b * ROWS, ROWS)], cbuf.at[pl.ds(b * ROWS, ROWS)], c_sem.at[b]
        )
        for b in range(steps)
    ]
    for load in loads:
        load.start()

    def plane_id(r):
        return {"x": r // (NY * 2), "y": (r // 2) % NY, "core": r % 2}

    barrier = pltpu.get_barrier_semaphore()

    @pl.loop(1, NZ)
    def _(o):
        pl.semaphore_signal(barrier, inc=1, device_id={"group": (z + o) % NZ}, device_id_type=MESH)

    @pl.loop(1, PLANE)
    def _(o):
        pl.semaphore_signal(barrier, inc=1, device_id=plane_id((me + o) % PLANE), device_id_type=MESH)

    pl.semaphore_wait(barrier, NZ - 1 + PLANE - 1)

    def along(o):
        return pltpu.make_async_remote_copy(
            src_ref=q_ref, dst_ref=zbuf.at[z], send_sem=zs_sem.at[o], recv_sem=zr_sem.at[z],
            device_id={"group": (z + o) % NZ}, device_id_type=MESH,
        )

    def along_in(o):
        other = (z + o) % NZ
        return pltpu.make_async_remote_copy(
            src_ref=q_ref, dst_ref=zbuf.at[other], send_sem=zs_sem.at[o], recv_sem=zr_sem.at[other],
            device_id={"group": other}, device_id_type=MESH,
        )

    for o in range(1, NZ):
        along(o).start()
    zbuf[pl.ds(z, 1)] = q_ref[...][None]

    def source_row(slot):
        kind, da, db = slot
        cs = c if kind == "o" else 1 - c
        xs = (x + da * (1 - cs) + db * cs) % NX
        ys = (y + da * cs + db * (1 - cs)) % NY
        return (xs * NY + ys) * 2 + cs

    rows = [source_row(slot) for slot in SLOTS]
    for k in range(PLANE):
        trel[:, k * block : (k + 1) * block] = t_ref[rows[k]][:, :block]

    for o in range(1, NZ):
        along_in(o).wait_recv()
    qall[0:block, :] = jnp.concatenate(
        [zbuf[k].astype(jnp.float32) for k in range(NZ)], axis=0
    ).astype(qall.dtype)

    sent = []

    def at(slot):
        return qall.at[pl.ds(PLACE[slot] * block, block)]

    def copy(src, dst, device, sem):
        op = pltpu.make_async_remote_copy(
            src_ref=at(src), dst_ref=at(dst), send_sem=send_sem.at[len(sent)], recv_sem=sem,
            device_id=device, device_id_type=MESH,
        )
        op.start()
        sent.append(op)

    def over(src, ea, eb):
        _, da, db = src
        to = ("o", (da - ea) % 4, (db - eb) % 4)
        device = {
            "x": (x + ea * (1 - c) + eb * c) % NX,
            "y": (y + ea * c + eb * (1 - c)) % NY,
        }
        copy(src, to, device, own_sem.at[to[1] * 4 + to[2]])

    def across(src):
        _, da, db = src
        copy(src, ("m", da, db), {"core": 1 - c}, mate_sem.at[da * 4 + db])

    def arrived(slot):
        kind, da, db = slot
        sem = own_sem if kind == "o" else mate_sem
        pltpu.make_async_remote_copy(
            src_ref=at(slot), dst_ref=at(slot), send_sem=send_sem.at[0], recv_sem=sem.at[da * 4 + db],
            device_id={"core": 1 - c}, device_id_type=MESH,
        ).wait_recv()

    def passed_on(slot):
        kind, da, db = slot
        if kind == "m":
            return
        if db == 0:
            over(slot, 0, 1)
            over(slot, 0, -1)
        if db == 1 and da in (2, 3):
            over(slot, 0, -1)
        if db == 3 and da in (0, 1):
            over(slot, 0, 1)
        across(slot)

    mine = ("o", 0, 0)
    over(mine, 1, 0)
    over(mine, -1, 0)
    passed_on(mine)
    over(mine, 2, 0)

    def fresh():
        return (
            jnp.full((8, CHUNK), LOWEST, jnp.float32),
            jnp.zeros((8, CHUNK), jnp.float32),
            jnp.zeros((8, CHUNK), jnp.float32),
        )

    state = fresh()
    pending = None
    chunks = qall.shape[0] // CHUNK

    def drained(pending, state):
        k, b, side = pending
        mark = trel[:, k * CHUNK : (k + 1) * CHUNK] - base
        wanted = jnp.broadcast_to(mark >> 3, (8, CHUNK))
        state = folded(sbuf.at[side], ROWS // 8, *state, wanted, b * (ROWS // 8))
        if b < steps - 1:
            return state
        top, total, picked = state
        best = jnp.max(top, axis=0, keepdims=True)
        whole = jnp.sum(total * jnp.exp(top - best), axis=0, keepdims=True)
        line = lax.broadcasted_iota(jnp.int32, (8, CHUNK), 0)
        hit = jnp.where(line == (mark & 7), picked, 0.0)
        res[0:1, k * CHUNK : (k + 1) * CHUNK] = best + jnp.log(whole)
        res[1:2, k * CHUNK : (k + 1) * CHUNK] = jnp.sum(hit, axis=0, keepdims=True)
        return fresh()

    for k in range(chunks):
        for b in range(steps):
            if k == 0:
                loads[b].wait()
            for slot in ARRIVALS.get((k, b), ()):
                arrived(slot)
                passed_on(slot)
            side = (k * steps + b) % 2
            sbuf[side] = lax.dot_general(
                cbuf[b * ROWS : (b + 1) * ROWS, :], qall[k * CHUNK : (k + 1) * CHUNK, :],
                (((1,), (1,)), ((), ())), preferred_element_type=jnp.float32,
            )
            if pending is not None:
                state = drained(pending, state)
            pending = (k, b, side)
    drained(pending, state)

    for k in range(PLANE):
        part[rows[k], :, 0:block] = res[:, k * block : (k + 1) * block]

    def gathered(src, dst, s_sem, r_sem):
        def op(o, at_me):
            other = (me + o) % PLANE
            slot = me if at_me else other
            return pltpu.make_async_remote_copy(
                src_ref=src(other), dst_ref=dst.at[slot], send_sem=s_sem.at[o], recv_sem=r_sem.at[slot],
                device_id=plane_id(other), device_id_type=MESH,
            )

        @pl.loop(1, PLANE)
        def _(o):
            op(o, True).start()

        @pl.loop(1, PLANE)
        def _(o):
            op(o, False).wait_recv()

        return op

    inbox[pl.ds(me, 1)] = part[pl.ds(me, 1)]
    scattered = gathered(lambda other: part.at[other], inbox, rs_sem, rr_sem)
    lse, picked = merged(inbox[...])

    zin[pl.ds(z, 1), 0:1, :] = lse[None]
    zin[pl.ds(z, 1), 1:2, :] = picked[None]

    def reduce_to(o, at_me):
        other = (z + o) % NZ
        slot = z if at_me else other
        return pltpu.make_async_remote_copy(
            src_ref=zin.at[z], dst_ref=zin.at[slot], send_sem=gs_sem.at[o], recv_sem=gr_sem.at[slot],
            device_id={"group": other}, device_id_type=MESH,
        )

    for o in range(1, NZ):
        reduce_to(o, True).start()
    for o in range(1, NZ):
        reduce_to(o, False).wait_recv()
    lse, picked = merged(zin[...])

    outall[pl.ds(me, 1)] = (lse - picked)[None]
    spread = gathered(lambda other: outall.at[me], outall, as_sem, ar_sem)
    out_ref[...] = outall[...]

    for o in range(1, NZ):
        along(o).wait_send()
        reduce_to(o, True).wait_send()
    for op in sent:
        op.wait_send()

    @pl.loop(1, PLANE)
    def _(o):
        scattered(o, True).wait_send()
        spread(o, True).wait_send()


def on_device(queries, candidates, targets):
    per, width = queries.shape
    block = NZ * per
    total = block * PLANE
    marks = targets.reshape(NZ, PLANE, per).transpose(1, 0, 2).reshape(PLANE, 1, block)
    marks = jnp.pad(marks, ((0, 0), (0, 0), (0, LANES - block)))
    DMA = pltpu.SemaphoreType.DMA
    out = pl.pallas_call(
        kernel,
        out_shape=jax.ShapeDtypeStruct((PLANE, 1, LANES), jnp.float32),
        in_specs=[
            pl.BlockSpec(memory_space=pltpu.VMEM),
            pl.BlockSpec(memory_space=pltpu.VMEM),
            pl.BlockSpec(memory_space=pl.ANY),
        ],
        out_specs=pl.BlockSpec(memory_space=pltpu.VMEM),
        scratch_shapes=[
            pltpu.VMEM((NZ, per, width), jnp.bfloat16),
            pltpu.VMEM((total, width), jnp.bfloat16),
            pltpu.VMEM(candidates.shape, jnp.bfloat16),
            pltpu.VMEM((2, ROWS, CHUNK), jnp.float32),
            pltpu.VMEM((1, total), jnp.int32),
            pltpu.VMEM((2, total), jnp.float32),
            pltpu.VMEM((PLANE, 2, LANES), jnp.float32),
            pltpu.VMEM((PLANE, 2, LANES), jnp.float32),
            pltpu.VMEM((NZ, 2, LANES), jnp.float32),
            pltpu.VMEM((PLANE, 1, LANES), jnp.float32),
            DMA((candidates.shape[0] // ROWS,)),
            DMA((NZ,)),
            DMA((NZ,)),
            DMA((31,)),
            DMA((16,)),
            DMA((16,)),
            DMA((PLANE,)),
            DMA((PLANE,)),
            DMA((NZ,)),
            DMA((NZ,)),
            DMA((PLANE,)),
            DMA((PLANE,)),
        ],
        compiler_params=pltpu.CompilerParams(
            collective_id=0, has_side_effects=True, vmem_limit_bytes=56 * 2**20
        ),
    )(queries, marks, candidates)
    losses = out[:, 0, :block].reshape(PLANE, NZ, per).transpose(1, 0, 2).reshape(total)
    return losses, jnp.mean(losses)


def solution(mesh):
    finer = Mesh(mesh.devices.reshape(mesh.shape["group"], NX, NY, 2), EVERY)
    return jax.shard_map(
        on_device,
        mesh=finer,
        in_specs=(P(EVERY, None), P(EVERY, None), P()),
        out_specs=(P(), P()),
        check_vma=False,
    )
```

time: 196 us -> 68.1 us (0.35)
  blocking collectives: 71.9 us -> 0 us
  Pallas kernels: 0 us -> 61.3 us
  waiting for transfers between devices: 40.6 us -> 0 us
  local copies, waits for them, and re-layouts: 31.7 us -> 2.6 us
  matrix products: 21.4 us -> 0 us
  between operations: 16.2 us -> 2.44 us
  other arithmetic: 13.4 us -> 1.36 us
    pallas_call x0 -> x1, Pallas kernels: none -> 61.3 us  [on_device(): pl.pallas_call(kernel, out_shape=jax.ShapeDtypeStruct((PLANE, 1, LANES),...]
    all_gather x2 -> x0, waiting for transfers between devices: 40.6 us -> none  [gather_in_order(): tiles = lax.all_gather(tiles, axes[k], axis=0, tiled=True)]
    all_to_all x2 -> x0, blocking collectives: 38.3 us -> none  [from_everyone(): return lax.all_to_all(copies, axis, split_axis=0, concat_axis=0, tiled=True)]
    all_gather x2 -> x0, blocking collectives: 33.7 us -> none  [gather_in_order(): tiles = lax.all_gather(tiles, axes[k], axis=0, tiled=True)]
    dot_general x3 -> x0, matrix products: 21.4 us -> none  [score_panel(): scores = jnp.dot(panel, candidates.T, preferred_element_type=jnp.float32)]
    gather x2 -> x0, local copies, waits for them, and re-layouts: 14.5 us -> none  [score_rows(): chosen = jnp.take(candidates, jnp.clip(local, 0, rows - 1), axis=0)]
    reduce_sum x4 -> x0, other arithmetic: 11.6 us -> none  [the longest x1 7.8 us: score_rows(): jnp.sum(piece.astype(jnp.float32) * chosen.astype(jnp.float32), axis=1)]
    another operation x1, local copies, waits for them, and re-layouts: 4.87 us -> 0.01 us  [on_device(): out[:, 0, :block].reshape(PLANE, NZ, per).transpose(1, 0, 2).reshape(total)]
  transfers between devices with their start and end apart: 2 -> 0, of which waited for: 2 -> 0; matrix products, arithmetic and copies ran while one was open for 8% -> 0% of each run, Pallas kernels for 0% -> 0%
where the time goes in v1:
time: 68.1 us; the launch traced here: 67.7 us
  Pallas kernels  61.3 us (90%)
  local copies, waits for them, and re-layouts  2.6 us (4%)
  between operations  2.44 us (4%)
  other arithmetic  1.36 us (2%)
    pallas_call x1, Pallas kernels, on_device(): pl.pallas_call(kernel, out_shape=jax.ShapeDtypeStruct((PLANE, 1, LANES),...  61.3 us

profile of v1, /device:TPU:1, one launch (start us, length us, event | category | flops | bytes accessed | tf_op | source)
XLA Modules:
  0.0 67.7 jit_solution(13745303589394557294)
XLA Ops:
  0.6 0.8 %reshape.13 = s32[8,32,6]{2,1,0:T(8,128)S(1)} reshape(s32[1536]{0:T(1024)} %param.5) | data formatting | bytes 12288 | tf_op jit(solution)/shard_map/reshape | solution.py:298
  1.5 0.1 copy.5
  1.6 0.1 copy.6
  1.7 0.6 pad.4.t_ref
  2.3 61.3 %shard_map.50 = f32[32,1,128]{2,1,0:T(1,128)} custom-call(bf16[6,1024]{1,0:T(8,128)(2,1)} %q_ref.1, s32[32,1,128]{2,1,0:T(1,128)} %pad.4.t_ref, bf16[4096,1024]{1,0:T(8,128)(2,1)} %c_hbm.1), custom_call_target="tpu_custom_call" | custom-call | tf_op jit(solution)/shard_map/pallas_call | solution.py:301
  63.6 1.4 %slice_reduce_fusion = (f32[]{:T(128)}, f32[32,1,48]{2,1,0:T(1,128)S(1)}) fusion(f32[32,1,128]{2,1,0:T(1,128)} %shard_map.50), kind=kLoop, calls=%fused_computation | loop fusion | flops 1535 | bytes 12292 | tf_op jit(solution)/shard_map/reduce_sum | solution.py:339
  65.6 0.1 copy.7
  65.7 0.1 copy.8
  65.8 0.7 %reshape.15 = f32[1536]{0:T(1024)} reshape(f32[8,32,6]{2,1,0:T(8,128)S(1)} %copy.8) | data formatting | bytes 12288 | tf_op jit(solution)/shard_map/reshape | solution.py:338
  (2 shorter events, 0.0 us)

commit v2 on v1

--- a/solution.py
+++ b/solution.py
@@ -17,6 +17,11 @@
 CHUNK = 256
 ROWS = 1024
 LOWEST = -3.0e38
+AROUND = sorted(
+    ((dx, dy, dc) for dx in range(NX) for dy in range(NY) for dc in range(2) if dx or dy or dc),
+    key=lambda d: -(min(d[0], NX - d[0]) + min(d[1], NY - d[1])),
+)
+ALONG = sorted(range(1, NZ), key=lambda o: -min(o, NZ - o))
 
 SLOTS = (
     ("o", 0, 0), ("o", 1, 0), ("o", 3, 0), ("o", 0, 1), ("o", 0, 3), ("m", 0, 0),
@@ -64,24 +69,25 @@
 
 
 def kernel(
-    q_ref, t_ref, c_hbm, out_ref,
-    zbuf, qall, cbuf, sbuf, trel, res, part, inbox, zin, outall,
+    q_ref, t_ref, c_hbm, out_ref, mean_ref,
+    zbuf, qall, cbuf, sbuf, pmat, own, tbuf, trel, res, part, inbox, zin, outall,
     c_sem, zs_sem, zr_sem, send_sem, own_sem, mate_sem,
     rs_sem, rr_sem, gs_sem, gr_sem, as_sem, ar_sem,
 ):
     z, x, y, c = (lax.axis_index(a) for a in EVERY)
     per = q_ref.shape[0]
     block = NZ * per
-    n_cand = cbuf.shape[0]
+    n_cand = cbuf.shape[1]
+    tiles = cbuf.shape[0]
     steps = n_cand // ROWS
     me = (x * NY + y) * 2 + c
     base = (z * PLANE + me) * n_cand
 
     loads = [
         pltpu.make_async_copy(
-            c_hbm.at[pl.ds(b * ROWS, ROWS)], cbuf.at[pl.ds(b * ROWS, ROWS)], c_sem.at[b]
-        )
-        for b in range(steps)
+            c_hbm.at[:, pl.ds(j * LANES, LANES)], cbuf.at[j], c_sem.at[j]
+        )
+        for j in range(tiles)
     ]
     for load in loads:
         load.start()
@@ -99,24 +105,28 @@
     def _(o):
         pl.semaphore_signal(barrier, inc=1, device_id=plane_id((me + o) % PLANE), device_id_type=MESH)
 
-    pl.semaphore_wait(barrier, NZ - 1 + PLANE - 1)
-
-    def along(o):
-        return pltpu.make_async_remote_copy(
-            src_ref=q_ref, dst_ref=zbuf.at[z], send_sem=zs_sem.at[o], recv_sem=zr_sem.at[z],
-            device_id={"group": (z + o) % NZ}, device_id_type=MESH,
-        )
-
-    def along_in(o):
-        other = (z + o) % NZ
-        return pltpu.make_async_remote_copy(
-            src_ref=q_ref, dst_ref=zbuf.at[other], send_sem=zs_sem.at[o], recv_sem=zr_sem.at[other],
-            device_id={"group": other}, device_id_type=MESH,
-        )
-
-    for o in range(1, NZ):
-        along(o).start()
-    zbuf[pl.ds(z, 1)] = q_ref[...][None]
+    count = t_ref.shape[1]
+    g = lax.broadcasted_iota(jnp.int32, (1, count), 1).astype(jnp.float32)
+    gz = jnp.floor((2.0 * g + 1.0) * (0.5 / (PLANE * per)))
+    within = g - gz * (PLANE * per)
+    row = jnp.floor((2.0 * within + 1.0) * (0.5 / per))
+    lane = (gz * per + within - row * per).astype(jnp.int32)
+    row = row.astype(jnp.int32)
+    at_lane = lax.broadcasted_iota(jnp.int32, (LANES, count), 0) == lane
+    pmat[...] = jnp.where(at_lane, 1.0, 0.0).astype(pmat.dtype)
+    at_row = lax.broadcasted_iota(jnp.int32, (PLANE, count), 0) == row
+    own[...] = jnp.where(at_row, 1.0, 0.0)
+
+    t = t_ref[...]
+    pieces = jnp.concatenate(
+        [own[...] * p.astype(jnp.float32) for p in (t & 255, (t >> 8) & 255, t >> 16)], axis=0
+    ).astype(pmat.dtype)
+    table = lax.dot_general(
+        pieces, pmat[...], (((1,), (1,)), ((), ())), preferred_element_type=jnp.float32
+    )
+    tbuf[...] = (
+        table[0:PLANE] + 256.0 * table[PLANE : 2 * PLANE] + 65536.0 * table[2 * PLANE :]
+    ).astype(jnp.int32)
 
     def source_row(slot):
         kind, da, db = slot
@@ -127,18 +137,39 @@
 
     rows = [source_row(slot) for slot in SLOTS]
     for k in range(PLANE):
-        trel[:, k * block : (k + 1) * block] = t_ref[rows[k]][:, :block]
-
-    for o in range(1, NZ):
+        trel[:, k * block : (k + 1) * block] = tbuf[pl.ds(rows[k], 1), :][:, :block]
+
+    pl.semaphore_wait(barrier, NZ - 1 + PLANE - 1)
+
+    def along(o):
+        return pltpu.make_async_remote_copy(
+            src_ref=q_ref, dst_ref=zbuf.at[z], send_sem=zs_sem.at[o], recv_sem=zr_sem.at[z],
+            device_id={"group": (z + o) % NZ}, device_id_type=MESH,
+        )
+
+    def along_in(o):
+        other = (z + o) % NZ
+        return pltpu.make_async_remote_copy(
+            src_ref=q_ref, dst_ref=zbuf.at[other], send_sem=zs_sem.at[o], recv_sem=zr_sem.at[other],
+            device_id={"group": other}, device_id_type=MESH,
+        )
+
+    for o in ALONG:
+        along(o).start()
+    zbuf[pl.ds(z, 1)] = q_ref[...][None]
+
+    for o in ALONG:
         along_in(o).wait_recv()
-    qall[0:block, :] = jnp.concatenate(
+    column = jnp.concatenate(
         [zbuf[k].astype(jnp.float32) for k in range(NZ)], axis=0
     ).astype(qall.dtype)
+    for j in range(tiles):
+        qall[0, j] = column[:, j * LANES : (j + 1) * LANES]
 
     sent = []
 
     def at(slot):
-        return qall.at[pl.ds(PLACE[slot] * block, block)]
+        return qall.at[PLACE[slot]]
 
     def copy(src, dst, device, sem):
         op = pltpu.make_async_remote_copy(
@@ -183,10 +214,10 @@
         across(slot)
 
     mine = ("o", 0, 0)
+    over(mine, 2, 0)
     over(mine, 1, 0)
     over(mine, -1, 0)
     passed_on(mine)
-    over(mine, 2, 0)
 
     def fresh():
         return (
@@ -197,7 +228,23 @@
 
     state = fresh()
     pending = None
-    chunks = qall.shape[0] // CHUNK
+    chunks = PLANE * block // CHUNK
+    groups = block // 16
+
+    def candidates_of(b):
+        return jnp.concatenate(
+            [cbuf[j, b * ROWS : (b + 1) * ROWS, :] for j in range(tiles)], axis=1
+        )
+
+    def queries_of(k):
+        places = [divmod(k * CHUNK // 16 + i, groups) for i in range(CHUNK // 16)]
+        return jnp.concatenate(
+            [
+                jnp.concatenate([qall[p, j, 16 * i : 16 * i + 16, :] for p, i in places], axis=0)
+                for j in range(tiles)
+            ],
+            axis=1,
+        )
 
     def drained(pending, state):
         k, b, side = pending
@@ -215,16 +262,16 @@
         res[1:2, k * CHUNK : (k + 1) * CHUNK] = jnp.sum(hit, axis=0, keepdims=True)
         return fresh()
 
+    for load in loads:
+        load.wait()
     for k in range(chunks):
         for b in range(steps):
-            if k == 0:
-                loads[b].wait()
             for slot in ARRIVALS.get((k, b), ()):
                 arrived(slot)
                 passed_on(slot)
             side = (k * steps + b) % 2
             sbuf[side] = lax.dot_general(
-                cbuf[b * ROWS : (b + 1) * ROWS, :], qall[k * CHUNK : (k + 1) * CHUNK, :],
+                candidates_of(b), queries_of(k),
                 (((1,), (1,)), ((), ())), preferred_element_type=jnp.float32,
             )
             if pending is not None:
@@ -236,23 +283,22 @@
         part[rows[k], :, 0:block] = res[:, k * block : (k + 1) * block]
 
     def gathered(src, dst, s_sem, r_sem):
-        def op(o, at_me):
-            other = (me + o) % PLANE
-            slot = me if at_me else other
-            return pltpu.make_async_remote_copy(
-                src_ref=src(other), dst_ref=dst.at[slot], send_sem=s_sem.at[o], recv_sem=r_sem.at[slot],
-                device_id=plane_id(other), device_id_type=MESH,
+        ops = []
+        for k, (dx, dy, dc) in enumerate(AROUND):
+            device = {"x": (x + dx) % NX, "y": (y + dy) % NY, "core": (c + dc) % 2}
+            other = (device["x"] * NY + device["y"]) * 2 + device["core"]
+            op, back = (
+                pltpu.make_async_remote_copy(
+                    src_ref=src(other), dst_ref=dst.at[slot], send_sem=s_sem.at[k],
+                    recv_sem=r_sem.at[slot], device_id=device, device_id_type=MESH,
+                )
+                for slot in (me, other)
             )
-
-        @pl.loop(1, PLANE)
-        def _(o):
-            op(o, True).start()
-
-        @pl.loop(1, PLANE)
-        def _(o):
-            op(o, False).wait_recv()
-
-        return op
+            op.start()
+            ops.append((op, back))
+        for _, back in ops:
+            back.wait_recv()
+        return ops
 
     inbox[pl.ds(me, 1)] = part[pl.ds(me, 1)]
     scattered = gathered(lambda other: part.at[other], inbox, rs_sem, rr_sem)
@@ -269,56 +315,74 @@
             device_id={"group": other}, device_id_type=MESH,
         )
 
-    for o in range(1, NZ):
+    for o in ALONG:
         reduce_to(o, True).start()
-    for o in range(1, NZ):
+    for o in ALONG:
         reduce_to(o, False).wait_recv()
     lse, picked = merged(zin[...])
 
     outall[pl.ds(me, 1)] = (lse - picked)[None]
     spread = gathered(lambda other: outall.at[me], outall, as_sem, ar_sem)
-    out_ref[...] = outall[...]
-
-    for o in range(1, NZ):
+    lanes = lax.broadcasted_iota(jnp.int32, (PLANE, LANES), 1)
+    value = jnp.concatenate([outall[k] for k in range(PLANE)], axis=0)
+    value = jnp.where(lanes < block, value, 0.0)
+    high = value.astype(pmat.dtype)
+    rest = value - high.astype(jnp.float32)
+    middle = rest.astype(pmat.dtype)
+    low = (rest - middle.astype(jnp.float32)).astype(pmat.dtype)
+    spreads = jnp.dot(
+        jnp.concatenate([high, middle, low], axis=0), pmat[...], preferred_element_type=jnp.float32
+    )
+    value = spreads[0:PLANE] + spreads[PLANE : 2 * PLANE] + spreads[2 * PLANE :]
+    losses = jnp.sum(own[...] * value, axis=0, keepdims=True)
+    out_ref[...] = losses
+    mean_ref[0, 0] = jnp.sum(losses) / count
+
+    for o in ALONG:
         along(o).wait_send()
         reduce_to(o, True).wait_send()
     for op in sent:
         op.wait_send()
 
-    @pl.loop(1, PLANE)
-    def _(o):
-        scattered(o, True).wait_send()
-        spread(o, True).wait_send()
+    for op, _ in scattered + spread:
+        op.wait_send()
 
 
 def on_device(queries, candidates, targets):
     per, width = queries.shape
     block = NZ * per
     total = block * PLANE
-    marks = targets.reshape(NZ, PLANE, per).transpose(1, 0, 2).reshape(PLANE, 1, block)
-    marks = jnp.pad(marks, ((0, 0), (0, 0), (0, LANES - block)))
     DMA = pltpu.SemaphoreType.DMA
-    out = pl.pallas_call(
+    losses, mean = pl.pallas_call(
         kernel,
-        out_shape=jax.ShapeDtypeStruct((PLANE, 1, LANES), jnp.float32),
+        out_shape=(
+            jax.ShapeDtypeStruct((1, total), jnp.float32),
+            jax.ShapeDtypeStruct((1, 1), jnp.float32),
+        ),
         in_specs=[
             pl.BlockSpec(memory_space=pltpu.VMEM),
             pl.BlockSpec(memory_space=pltpu.VMEM),
             pl.BlockSpec(memory_space=pl.ANY),
         ],
-        out_specs=pl.BlockSpec(memory_space=pltpu.VMEM),
+        out_specs=(
+            pl.BlockSpec(memory_space=pltpu.VMEM),
+            pl.BlockSpec(memory_space=pltpu.SMEM),
+        ),
         scratch_shapes=[
             pltpu.VMEM((NZ, per, width), jnp.bfloat16),
-            pltpu.VMEM((total, width), jnp.bfloat16),
-            pltpu.VMEM(candidates.shape, jnp.bfloat16),
+            pltpu.VMEM((PLANE, width // LANES, block, LANES), jnp.bfloat16),
+            pltpu.VMEM((width // LANES, candidates.shape[0], LANES), jnp.bfloat16),
             pltpu.VMEM((2, ROWS, CHUNK), jnp.float32),
+            pltpu.VMEM((LANES, total), jnp.bfloat16),
+            pltpu.VMEM((PLANE, total), jnp.float32),
+            pltpu.VMEM((PLANE, LANES), jnp.int32),
             pltpu.VMEM((1, total), jnp.int32),
             pltpu.VMEM((2, total), jnp.float32),
             pltpu.VMEM((PLANE, 2, LANES), jnp.float32),
             pltpu.VMEM((PLANE, 2, LANES), jnp.float32),
             pltpu.VMEM((NZ, 2, LANES), jnp.float32),
             pltpu.VMEM((PLANE, 1, LANES), jnp.float32),
-            DMA((candidates.shape[0] // ROWS,)),
+            DMA((width // LANES,)),
             DMA((NZ,)),
             DMA((NZ,)),
             DMA((31,)),
@@ -334,9 +398,8 @@
         compiler_params=pltpu.CompilerParams(
             collective_id=0, has_side_effects=True, vmem_limit_bytes=56 * 2**20
         ),
-    )(queries, marks, candidates)
-    losses = out[:, 0, :block].reshape(PLANE, NZ, per).transpose(1, 0, 2).reshape(total)
-    return losses, jnp.mean(losses)
+    )(queries, targets.reshape(1, total), candidates)
+    return losses.reshape(total), mean.reshape(())
 
 
 def solution(mesh):

time: 68.1 us -> 63.2 us (0.928)
  Pallas kernels: 61.3 us -> 57.9 us
  local copies, waits for them, and re-layouts: 2.6 us -> 1.29 us
    pallas_call x1, Pallas kernels: 61.3 us -> 57.9 us  [on_device(): pl.pallas_call(kernel, out_shape=(jax.ShapeDtypeStruct((1, total), jnp.fl...]
    reduce_sum x1 -> x0, other arithmetic: 1.36 us -> none  [on_device(): return (losses, jnp.mean(losses))]
    pallas_call x0 -> x1, other arithmetic: none -> 1.31 us  [on_device(): pl.pallas_call(kernel, out_shape=(jax.ShapeDtypeStruct((1, total), jnp.fl...]
    reshape x4 -> x1, local copies, waits for them, and re-layouts: 1.65 us -> 1.29 us  [on_device(): targets.reshape(1, total)]
where the time goes in v2:
time: 63.2 us; the launch traced here: 62.8 us
  Pallas kernels  57.9 us (92%)
  between operations  2.33 us (4%)
  other arithmetic  1.31 us (2%)
  local copies, waits for them, and re-layouts  1.29 us (2%)
    pallas_call x1, Pallas kernels, on_device(): pl.pallas_call(kernel, out_shape=(jax.ShapeDtypeStruct((1, total), jnp.fl...  57.9 us
    pallas_call x1, other arithmetic, on_device(): pl.pallas_call(kernel, out_shape=(jax.ShapeDtypeStruct((1, total), jnp.fl...  1.31 us
    reshape x1, local copies, waits for them, and re-layouts, on_device(): targets.reshape(1, total)  1.29 us

profile of v2, /device:TPU:1, one launch (start us, length us, event | category | flops | bytes accessed | tf_op | source)
XLA Modules:
  0.0 62.8 jit_solution(8555229979798996833)
XLA Ops:
  0.6 1.3 %reshape.13.t_ref = s32[1,1536]{1,0:T(1,128)} reshape(s32[1536]{0:T(1024)} %param.5) | data formatting | bytes 12288 | tf_op jit(solution)/shard_map/reshape | solution.py:401
  1.9 57.9 %shard_map.50 = (f32[1,1536]{1,0:T(1,128)}, f32[1,1]{1,0:T(1,128)}) custom-call(bf16[6,1024]{1,0:T(8,128)(2,1)} %q_ref.1, s32[1,1536]{1,0:T(1,128)} %reshape.13.t_ref, bf16[4096,1024]{1,0:T(8,128)(2,1)} %c_hbm.1), custom_call_target="tpu_custom_call" | custom-call | tf_op jit(solution)/shard_map/pallas_call | solution.py:356
  59.8 1.3 %reduce = f32[1536]{0:T(1024)} reduce(f32[1,1536]{1,0:T(1,128)} %get-tuple-element.4, f32[]{:T(128)} %constant.1), dimensions={0}, to_apply=%get-tuple-element.4.reduce_sub_computation | reduce | bytes 12292 | tf_op jit(solution)/shard_map/pallas_call | solution.py:356

commit v3 on v2

--- a/solution.py
+++ b/solution.py
@@ -24,26 +24,26 @@
 ALONG = sorted(range(1, NZ), key=lambda o: -min(o, NZ - o))
 
 SLOTS = (
-    ("o", 0, 0), ("o", 1, 0), ("o", 3, 0), ("o", 0, 1), ("o", 0, 3), ("m", 0, 0),
-    ("o", 2, 0), ("m", 1, 0), ("m", 3, 0), ("m", 0, 1), ("m", 0, 3),
+    ("o", 0, 0), ("m", 0, 0), ("o", 1, 0), ("o", 3, 0), ("m", 1, 0), ("m", 3, 0),
+    ("o", 0, 1), ("o", 0, 3), ("m", 0, 1), ("m", 0, 3), ("o", 2, 0),
     ("m", 2, 0), ("o", 1, 1), ("o", 3, 1), ("o", 1, 3), ("o", 3, 3),
     ("o", 2, 1), ("o", 2, 3), ("m", 1, 1), ("m", 3, 1), ("m", 1, 3), ("m", 3, 3),
-    ("m", 2, 1), ("m", 2, 3), ("o", 0, 2), ("o", 1, 2), ("o", 2, 2),
-    ("o", 3, 2), ("m", 0, 2), ("m", 1, 2), ("m", 2, 2), ("m", 3, 2),
+    ("m", 2, 1), ("m", 2, 3), ("o", 0, 2), ("o", 1, 2), ("m", 0, 2),
+    ("o", 3, 2), ("m", 1, 2), ("o", 2, 2), ("m", 3, 2), ("m", 2, 2),
 )
 PLACE = {slot: k for k, slot in enumerate(SLOTS)}
 ARRIVALS = {
-    (0, 0): (("o", 1, 0), ("o", 3, 0), ("o", 0, 1), ("o", 0, 3), ("m", 0, 0)),
-    (0, 2): (("o", 2, 0),),
-    (1, 0): (("m", 1, 0), ("m", 3, 0), ("m", 0, 1), ("m", 0, 3)),
+    (0, 0): (("o", 1, 0), ("o", 3, 0), ("m", 1, 0), ("m", 3, 0)),
+    (0, 2): (("o", 0, 1), ("o", 0, 3)),
+    (1, 0): (("m", 0, 1), ("m", 0, 3), ("o", 2, 0)),
     (1, 2): (("o", 1, 1), ("o", 3, 1), ("o", 1, 3), ("o", 3, 3)),
     (2, 0): (("m", 2, 0),),
-    (2, 2): (("o", 2, 1), ("o", 2, 3)),
+    (2, 2): (("o", 0, 2), ("o", 2, 1), ("o", 2, 3)),
     (3, 0): (("m", 1, 1), ("m", 3, 1), ("m", 1, 3), ("m", 3, 3)),
-    (3, 2): (("o", 0, 2), ("o", 1, 2)),
-    (4, 0): (("m", 2, 1), ("m", 2, 3), ("o", 2, 2)),
-    (4, 2): (("o", 3, 2),),
-    (5, 0): (("m", 0, 2), ("m", 1, 2), ("m", 2, 2), ("m", 3, 2)),
+    (3, 2): (("o", 1, 2), ("o", 3, 2)),
+    (4, 0): (("m", 2, 1), ("m", 2, 3), ("m", 0, 2)),
+    (4, 2): (("o", 2, 2),),
+    (5, 0): (("m", 1, 2), ("m", 3, 2), ("m", 2, 2)),
 }
 
 
@@ -204,6 +204,7 @@
         kind, da, db = slot
         if kind == "m":
             return
+        across(slot)
         if db == 0:
             over(slot, 0, 1)
             over(slot, 0, -1)
@@ -211,13 +212,15 @@
             over(slot, 0, -1)
         if db == 3 and da in (0, 1):
             over(slot, 0, 1)
-        across(slot)
 
     mine = ("o", 0, 0)
-    over(mine, 2, 0)
     over(mine, 1, 0)
     over(mine, -1, 0)
-    passed_on(mine)
+    across(mine)
+    arrived(("m", 0, 0))
+    over(mine, 0, 1)
+    over(mine, 0, -1)
+    over(mine, 2, 0)
 
     def fresh():
         return (

time: 63.2 us -> 62.7 us (level)
  no operation moved by 1% of the time
where the time goes in v3:
time: 62.7 us; the launch traced here: 62.3 us
  Pallas kernels  57.4 us (92%)
  between operations  2.33 us (4%)
  other arithmetic  1.31 us (2%)
  local copies, waits for them, and re-layouts  1.29 us (2%)
    pallas_call x1, Pallas kernels, on_device(): pl.pallas_call(kernel, out_shape=(jax.ShapeDtypeStruct((1, total), jnp.fl...  57.4 us
    pallas_call x1, other arithmetic, on_device(): pl.pallas_call(kernel, out_shape=(jax.ShapeDtypeStruct((1, total), jnp.fl...  1.31 us
    reshape x1, local copies, waits for them, and re-layouts, on_device(): targets.reshape(1, total)  1.29 us

profile of v3, /device:TPU:1, one launch (start us, length us, event | category | flops | bytes accessed | tf_op | source)
XLA Modules:
  0.0 62.3 jit_solution(3641082898877750602)
XLA Ops:
  0.6 1.3 %reshape.13.t_ref = s32[1,1536]{1,0:T(1,128)} reshape(s32[1536]{0:T(1024)} %param.5) | data formatting | bytes 12288 | tf_op jit(solution)/shard_map/reshape | solution.py:404
  1.9 57.4 %shard_map.50 = (f32[1,1536]{1,0:T(1,128)}, f32[1,1]{1,0:T(1,128)}) custom-call(bf16[6,1024]{1,0:T(8,128)(2,1)} %q_ref.1, s32[1,1536]{1,0:T(1,128)} %reshape.13.t_ref, bf16[4096,1024]{1,0:T(8,128)(2,1)} %c_hbm.1), custom_call_target="tpu_custom_call" | custom-call | tf_op jit(solution)/shard_map/pallas_call | solution.py:359
  59.3 1.3 %reduce = f32[1536]{0:T(1024)} reduce(f32[1,1536]{1,0:T(1,128)} %get-tuple-element.4, f32[]{:T(128)} %constant.1), dimensions={0}, to_apply=%get-tuple-element.4.reduce_sub_computation | reduce | bytes 12292 | tf_op jit(solution)/shard_map/pallas_call | solution.py:359
